TPU v7x, 32 devices: a whole 2x2x4 slice. The times are simulated.
32 devices in a mesh: gx: 2 (over core), gy: 4 (over y, x), gz: 4 (over z).
Axes of the slice: x: 2, y: 2, z: 4, core: 2. Of those that a mesh axis runs over, the one named last changes fastest.
Arguments:
- block_values: bfloat16 [4, 64, 4, 6, 128, 128], P('gy', 'gx', 'gz'), as said below
- block_cols: int32 [4, 64, 4, 6], P('gy', 'gx', 'gz'), may hold values from 0 to 63, as said below
Outputs:
- purified: float32 [256, 32768], P(('gx', 'gy'), 'gz')
Inputs may be any that keep to these rules, and one draw needn't show every extreme that they name: block_cols[a, s, b, :] holds 6 distinct tile columns of panel b at which tile row a * 64 + s of P is nonzero; every tile column of a panel is listed by exactly 6 tile rows of each slab; the pattern is symmetric: tile (i, j) is listed exactly when tile (j, i) is. `block_values`: P is symmetric: the tile listed at (i, j) is the transpose of the tile listed at (j, i), and diagonal tiles are symmetric.
All inputs are finite; a program needn't handle non-finite values.
Results may differ from a plain program's by a relative error of at most 0.0033.
Values may be sent and summed in bfloat16 or wider, within the bound.
A program may use at most 128 MiB of HBM per device.

v0:
```python
import jax
import jax.numpy as jnp
from jax import lax
from jax.sharding import PartitionSpec as P

WIN = 1


def broadcast(value, axis, source):
    kept = jnp.where(lax.axis_index(axis) == source, value, 0).astype(value.dtype)
    return lax.psum(kept, axis)


def densify(left_tiles, left_columns, slab_tiles):
    onehot = (
        left_columns[:, :, None] == jnp.arange(slab_tiles, dtype=jnp.int32)[None, None, :]
    ).astype(jnp.bfloat16)
    densified = jnp.einsum("wkj,wkyx->wyjx", onehot, left_tiles, preferred_element_type=jnp.float32)
    tile_size = left_tiles.shape[2]
    return densified.astype(jnp.bfloat16).reshape(
        left_tiles.shape[0] * tile_size, slab_tiles, tile_size
    )


def product_one(left_panel, panel_tiles, panel_columns):
    summed = jnp.zeros(
        (left_panel.shape[0], panel_tiles.shape[0], panel_tiles.shape[2]), jnp.float32
    )
    for column_slot in range(panel_tiles.shape[1]):
        picked = jnp.take(left_panel, panel_columns[:, column_slot], axis=1)
        summed = summed + jnp.einsum(
            "rix,iyx->riy", picked, panel_tiles[:, column_slot], preferred_element_type=jnp.float32
        )
    return summed


def product_two(rounded, panel_tiles, panel_columns, panel_width):
    summed = jnp.zeros((rounded.shape[0], panel_width, panel_tiles.shape[3]), jnp.float32)
    for column_slot in range(panel_tiles.shape[1]):
        product = jnp.einsum(
            "rix,ixy->riy", rounded, panel_tiles[:, column_slot], preferred_element_type=jnp.float32
        )
        summed = summed.at[:, panel_columns[:, column_slot], :].add(product)
    return summed


def local(block_values, block_cols):
    tiles_here = block_values[0, :, 0]
    columns_here = block_cols[0, :, 0]
    tile_size = tiles_here.shape[2]
    slab_tiles = tiles_here.shape[0] * lax.axis_size("gx")
    left_tiles, left_columns = (
        broadcast(tiles_here[:WIN], "gy", 0),
        broadcast(columns_here[:WIN], "gy", 0),
    )
    left_panel = densify(left_tiles, left_columns, slab_tiles)
    height = left_panel.shape[0]
    on_diagonal = (lax.axis_index("gy") == lax.axis_index("gz")).astype(jnp.float32)
    panel_tiles, panel_columns = (
        lax.all_gather(tiles_here, "gx", axis=0, tiled=True),
        lax.all_gather(columns_here, "gx", axis=0, tiled=True),
    )
    partial_square = product_one(left_panel, panel_tiles, panel_columns)
    partial_square = partial_square.reshape(height, slab_tiles * tile_size)
    square = lax.psum(partial_square, "gz")
    square_low = square.astype(jnp.bfloat16).reshape(height, slab_tiles, tile_size)
    applied = product_two(square_low, panel_tiles, panel_columns, slab_tiles).reshape(
        lax.axis_size("gy") * (height // lax.axis_size("gy")), slab_tiles * tile_size
    )
    return lax.psum_scatter(
        3.0 * on_diagonal * square - 2.0 * applied, "gy", scatter_dimension=0, tiled=True
    )


def solution(mesh):
    in_specs = (P("gy", "gx", "gz", None, None, None), P("gy", "gx", "gz", None))
    out_specs = P(("gx", "gy"), "gz")
    return jax.shard_map(local, mesh=mesh, in_specs=in_specs, out_specs=out_specs, check_vma=False)
```

profile of v0, /device:TPU:0, one launch (start us, length us, event | category | flops | bytes accessed | tf_op | source)
XLA Modules:
  0.0 449.8 jit_solution(1277576746980991775)
XLA Ops:
  9.2 8.0 %copy.48 = bf16[1,32,1,6,128,128]{5,4,1,3,2,0:T(8,128)(2,1)} copy(bf16[1,32,1,6,128,128]{5,4,3,2,1,0:T(8,128)(2,1)} %param.4) | data formatting | bytes 12582912 | tf_op args[0]
  18.2 8.9 %psum.25 = s32[6]{0:T(128)S(1)} all-reduce(s32[6]{0:T(128)S(1)} %fusion.44), channel_id=1, replica_groups=mesh['gx'=2,'gy'=4,'gz'=4] {'gy'}, use_global_device_ids=true, to_apply=%region_1.2 | all-reduce | flops 6 | bytes 48 | tf_op jit(solution)/shard_map/psum | solution.py:11
  29.5 27.4 %all-reduce.3.cloned.1.call-done = bf16[6,128,128]{2,0,1:T(8,128)(2,1)} async-done(((bf16[6,128,128]{2,0,1:T(8,128)(2,1)}), bf16[6,128,128]{2,0,1:T(8,128)(2,1)}) %all-reduce.3.cloned.1.call-update) | async-done | bytes 196624 | tf_op jit(solution)/shard_map/psum | solution.py:11
  73.0 6.2 %fusion.1 = f32[64,128,128]{1,2,0:T(8,128)} fusion(bf16[64,128,128]{2,1,0:T(8,128)(2,1)} %gather_fusion.4, pred[64]{0:T(512)(128)(4,1)S(1)} %get-tuple-element.24, bf16[64,6,128,128]{3,2,0,1:T(8,128)(2,1)} %bitcast.77), kind=kOutput, calls=%fused_computation.21 | convolution fusion | flops 269484032 | bytes 8388672 | tf_op jit(solution)/shard_map/rix,iyx->riy/dot_general | solution.py:31
  79.1 6.0 %fusion.3 = f32[64,128,128]{1,2,0:T(8,128)} fusion(bf16[64,128,128]{2,1,0:T(8,128)(2,1)} %gather_fusion.3, pred[64]{0:T(512)(128)(4,1)S(1)} %get-tuple-element.25, bf16[64,6,128,128]{3,2,0,1:T(8,128)(2,1)} %bitcast.78), kind=kOutput, calls=%fused_computation.23 | convolution fusion | flops 269484032 | bytes 8388672 | tf_op jit(solution)/shard_map/rix,iyx->riy/dot_general | solution.py:31
  85.2 3.6 fusion.5
  88.8 3.6 fusion.7
  92.4 3.6 fusion.9
  96.0 10.1 %add_add_fusion = f32[64,128,128]{1,2,0:T(8,128)} fusion(f32[64,128,128]{1,2,0:T(8,128)} %fusion.1, f32[64,128,128]{1,2,0:T(8,128)} %fusion.3, f32[64,128,128]{1,2,0:T(8,128)} %fusion.5, f32[64,128,128]{1,2,0:T(8,128)} %fusion.9, f32[64,128,128]{1,2,0:T(8,128)} %fusion.7, bf16[64,128,128]{2,1,0:T(8,128)(2,1)S(1)} %copy-done.4, ...), kind=kOutput, calls=%fused_computation.13 | convolution fusion | flops 274726912 | bytes 29360640 | tf_op jit(solution)/shard_map/rix,iyx->riy/dot_general | solution.py:31
  106.4 154.9 %all-reduce.5.cloned.1.call-done = f32[128,8192]{0,1:T(8,128)} async-done(((f32[128,8192]{0,1:T(8,128)}), f32[128,8192]{0,1:T(8,128)}) %all-reduce.5.cloned.1.call-update) | async-done | bytes 4194320 | tf_op jit(solution)/shard_map/psum | solution.py:65
  263.8 4.5 %fusion.24 = f32[64,128,128]{2,1,0:T(8,128)} fusion(bf16[128,64,128]{0,2,1:T(8,128)(2,1)S(1)} %bitcast.71, bf16[64,6,128,128]{3,2,0,1:T(8,128)(2,1)} %bitcast.79), kind=kOutput, calls=%fused_computation.46 | convolution fusion | flops 268435456 | bytes 8388608 | tf_op jit(solution)/shard_map/rix,ixy->riy/dot_general | solution.py:40
  268.4 4.6 %fusion.23 = f32[64,128,128]{2,1,0:T(8,128)} fusion(bf16[128,64,128]{0,2,1:T(8,128)(2,1)S(1)} %bitcast.72, bf16[64,6,128,128]{3,2,0,1:T(8,128)(2,1)} %bitcast.80), kind=kOutput, calls=%fused_computation.45 | convolution fusion | flops 268435456 | bytes 8388608 | tf_op jit(solution)/shard_map/rix,ixy->riy/dot_general | solution.py:40
  275.8 2.8 fusion.26
  286.7 13.9 %scatter_fusion = f32[128,64,128]{2,0,1:T(8,128)} fusion(f32[128,64,128]{2,0,1:T(8,128)} %broadcast_in_dim.30, s32[64]{0:T(128)S(1)} %get-tuple-element.7, f32[64,128,128]{2,1,0:T(8,128)} %fusion.23), kind=kCustom, calls=%fused_computation.6 | custom fusion | flops 1048576 | bytes 12583168 | tf_op jit(solution)/shard_map/scatter-add | solution.py:43
  300.6 13.6 %scatter_fusion.1 = f32[128,64,128]{2,0,1:T(8,128)} fusion(f32[128,64,128]{2,0,1:T(8,128)} %scatter_fusion, s32[64]{0:T(128)S(1)} %get-tuple-element.8, f32[64,128,128]{2,1,0:T(8,128)} %fusion.24), kind=kCustom, calls=%fused_computation.7 | custom fusion | flops 1048576 | bytes 12583168 | tf_op jit(solution)/shard_map/scatter-add | solution.py:43
  314.2 13.6 %scatter_fusion.2 = f32[128,64,128]{2,0,1:T(8,128)} fusion(f32[128,64,128]{2,0,1:T(8,128)} %scatter_fusion.1, s32[64]{0:T(128)S(1)} %get-tuple-element.9, f32[64,128,128]{2,1,0:T(8,128)} %fusion.25), kind=kCustom, calls=%fused_computation.8 | custom fusion | flops 1048576 | bytes 12583168 | tf_op jit(solution)/shard_map/scatter-add | solution.py:43
  327.9 13.7 %scatter_fusion.3 = f32[128,64,128]{2,0,1:T(8,128)} fusion(f32[128,64,128]{2,0,1:T(8,128)} %scatter_fusion.2, s32[64]{0:T(128)S(1)} %get-tuple-element.10, f32[64,128,128]{2,1,0:T(8,128)} %fusion.26), kind=kCustom, calls=%fused_computation.9 | custom fusion | flops 1048576 | bytes 12583168 | tf_op jit(solution)/shard_map/scatter-add | solution.py:43
  341.6 13.7 %scatter_fusion.4 = f32[128,64,128]{2,0,1:T(8,128)} fusion(f32[128,64,128]{2,0,1:T(8,128)} %scatter_fusion.3, s32[64]{0:T(128)S(1)} %get-tuple-element.11, f32[64,128,128]{2,1,0:T(8,128)} %fusion.27), kind=kCustom, calls=%fused_computation.10 | custom fusion | flops 1048576 | bytes 12583168 | tf_op jit(solution)/shard_map/scatter-add | solution.py:43
  355.2 13.6 %scatter_fusion.5 = f32[128,64,128]{2,0,1:T(8,128)} fusion(f32[128,64,128]{2,0,1:T(8,128)} %scatter_fusion.4, s32[64]{0:T(128)S(1)} %get-tuple-element.6, f32[64,128,128]{2,1,0:T(8,128)} %fusion.28), kind=kCustom, calls=%fused_computation.11 | custom fusion | flops 1048576 | bytes 12583168 | tf_op jit(solution)/shard_map/scatter-add | solution.py:43
  368.9 4.7 %broadcast_multiply_fusion = f32[128,64,128]{2,0,1:T(8,128)} fusion(f32[128,64,128]{2,0,1:T(8,128)} %scatter_fusion.5), kind=kLoop, calls=%fused_computation.37 | loop fusion | flops 1048576 | bytes 8388608 | tf_op jit(solution)/shard_map/mul | solution.py:71
  373.6 5.6 %copy.60 = f32[128,64,128]{0,2,1:T(8,128)} copy(f32[128,64,128]{2,0,1:T(8,128)} %broadcast_multiply_fusion) | data formatting | bytes 8388608 | tf_op jit(solution)/shard_map/mul | solution.py:71
  379.2 5.8 %bitcast_subtract_fusion = f32[128,8192]{0,1:T(8,128)} fusion(f32[128,64,128]{0,2,1:T(8,128)} %copy.60, f32[128,8192]{0,1:T(8,128)} %all-reduce.5.cloned.1.call-done, f32[]{:T(128)S(6)} %mul_shard_map.3), kind=kLoop, calls=%fused_computation.12 | loop fusion | flops 2097152 | bytes 12582916 | tf_op jit(solution)/shard_map/sub | solution.py:71
  385.1 5.6 %copy.68 = f32[128,8192]{1,0:T(8,128)} copy(f32[128,8192]{0,1:T(8,128)} %bitcast_subtract_fusion) | data formatting | bytes 8388608
  390.7 51.9 %reduce-scatter.4.cloned.1.call-done = f32[32,8192]{1,0:T(8,128)} async-done(((f32[128,8192]{1,0:T(8,128)}), f32[32,8192]{1,0:T(8,128)}) %reduce-scatter.4.cloned.1.call-update) | async-done | bytes 1048592 | tf_op jit(solution)/shard_map/reduce_scatter | solution.py:70
  (60 shorter events, 34.9 us)
Async XLA Ops:
  7.4 49.5 %all-reduce.3.cloned.1.call-start = ((), (), s32[]{:S(2)}) async-start(), calls=%async_computation.1 | async-start | bytes 524288 | tf_op jit(solution)/shard_map/psum | solution.py:11
  9.2 63.8 %all-gather.4.cloned.1.call-start = ((), (), s32[]{:S(2)}) async-start(), calls=%async_computation.3 | async-start | bytes 18874368 | tf_op jit(solution)/shard_map/all_gather | solution.py:60
  17.3 0.7 copy-start.5
  17.3 244.0 %all-reduce.5.cloned.1.call-start = ((), (), s32[]{:S(2)}) async-start(), calls=%async_computation.2 | async-start | bytes 8388608 | tf_op jit(solution)/shard_map/psum | solution.py:65
  73.0 12.2 %copy-start = (bf16[1,64,1,6,128,128]{5,4,1,3,2,0:T(8,128)(2,1)S(1)}, bf16[1,64,1,6,128,128]{5,4,1,3,2,0:T(8,128)(2,1)}, u32[]{:S(2)}) copy-start(bf16[1,64,1,6,128,128]{5,4,1,3,2,0:T(8,128)(2,1)} %all-gather.4.cloned.1.call-done) | copy-start | bytes 37748740
  79.1 6.0 %copy-start.3 = (bf16[64,128,128]{2,1,0:T(8,128)(2,1)S(1)}, bf16[64,128,128]{2,1,0:T(8,128)(2,1)}, u32[]{:S(2)}) copy-start(bf16[64,128,128]{2,1,0:T(8,128)(2,1)} %gather_fusion.2) | copy-start | bytes 6291460
  85.2 3.6 copy-start.2
  88.8 3.6 copy-start.1
  92.4 3.6 copy-start.4
  106.1 336.5 %reduce-scatter.4.cloned.1.call-start = ((), (), s32[]{:S(2)}) async-start(), calls=%async_computation.4 | async-start | bytes 5242880 | tf_op jit(solution)/shard_map/reduce_scatter | solution.py:70
  261.3 11.7 %slice-start = ((s8[12582912]{0:T(1024)(128)(4,1)}), s8[4194304]{0:T(1024)(128)(4,1)S(1)}, s32[]{:S(2)}) async-start(s8[12582912]{0:T(1024)(128)(4,1)} %bitcast.85), calls=%async_computation.5 | async-start | bytes 8388608
  263.8 9.1 %slice-start.1 = ((s8[12582912]{0:T(1024)(128)(4,1)}), s8[4194304]{0:T(1024)(128)(4,1)S(1)}, s32[]{:S(2)}) async-start(s8[12582912]{0:T(1024)(128)(4,1)} %bitcast.85), calls=%async_computation.6 | async-start | bytes 8388608
  268.3 4.6 %slice-start.2 = ((s8[12582912]{0:T(1024)(128)(4,1)}), s8[4194304]{0:T(1024)(128)(4,1)S(1)}, s32[]{:S(2)}) async-start(s8[12582912]{0:T(1024)(128)(4,1)} %bitcast.85), calls=%async_computation.7 | async-start | bytes 8388608
Sparse Core Ops, SparseCore 0:
  11.1 45.7 all-reduce.2
  106.3 154.9 all-reduce.4
  390.8 51.7 reduce-scatter.3
Sparse Core Ops, SparseCore 1:
  17.4 27.3 all-gather.3
where the time goes:
time: 451 us; the launch traced here: 450 us
  waiting for transfers between devices  234 us (52%)
  other arithmetic  96.8 us (21%)
  matrix products  55.3 us (12%)
  local copies, waits for them, and re-layouts  37.7 us (8%)
  between operations  14.7 us (3%)
  blocking collectives  10.7 us (2%)
    psum x1, waiting for transfers between devices, local(): square = lax.psum(partial_square, 'gz')  155 us
    scatter-add x6, other arithmetic, product_two(): summed = summed.at[:, panel_columns[:, column_slot], :].add(product)  82.2 us
    reduce_scatter x1, waiting for transfers between devices, local(): lax.psum_scatter(3.0 * on_diagonal * square - 2.0 * applied, 'gy', scatte...  51.9 us
    dot_general x6, matrix products, product_one(): jnp.einsum('rix,iyx->riy', picked, panel_tiles[:, column_slot], preferred...  33.1 us
    psum x1, waiting for transfers between devices, broadcast(): return lax.psum(kept, axis)  27.4 us
    dot_general x6, matrix products, product_two(): jnp.einsum('rix,ixy->riy', rounded, panel_tiles[:, column_slot], preferre...  20.4 us
    unnamed x21, local copies, waits for them, and re-layouts  14.4 us
    gather x6, local copies, waits for them, and re-layouts, product_one(): picked = jnp.take(left_panel, panel_columns[:, column_slot], axis=1)  12.9 us
  transfers between devices with their start and end apart: 4, of which 3 were waited for; matrix products, arithmetic and copies ran while one was open for 6% of the time, Pallas kernels for 0%

commit v1 on v0

--- a/solution.py
+++ b/solution.py
@@ -62,7 +62,9 @@
     )
     partial_square = product_one(left_panel, panel_tiles, panel_columns)
     partial_square = partial_square.reshape(height, slab_tiles * tile_size)
-    square = lax.psum(partial_square, "gz")
+    square = partial_square
+    for hop in (1, 2):
+        square = square + lax.ppermute(square, "gz", [(dev, dev ^ hop) for dev in range(4)])
     square_low = square.astype(jnp.bfloat16).reshape(height, slab_tiles, tile_size)
     applied = product_two(square_low, panel_tiles, panel_columns, slab_tiles).reshape(
         lax.axis_size("gy") * (height // lax.axis_size("gy")), slab_tiles * tile_size

time: 451 us -> 579 us (1.28)
  waiting for transfers between devices: 234 us -> 351 us
  other arithmetic: 96.8 us -> 104 us
    ppermute x0 -> x2, waiting for transfers between devices: none -> 270 us  [local(): lax.ppermute(square, 'gz', [(dev, dev ^ hop) for dev in range(4)])]
    psum x1 -> x0, waiting for transfers between devices: 155 us -> none  [local(): square = lax.psum(partial_square, 'gz')]
  transfers between devices with their start and end apart: 4 -> 5, of which waited for: 3 -> 4; matrix products, arithmetic and copies ran while one was open for 6% -> 4% of each run, Pallas kernels for 0% -> 0%
where the time goes in v1:
time: 579 us; the launch traced here: 578 us
  waiting for transfers between devices  351 us (61%)
  other arithmetic  104 us (18%)
  matrix products  55.8 us (10%)
  local copies, waits for them, and re-layouts  37.8 us (7%)
  between operations  15 us (3%)
  blocking collectives  10.7 us (2%)
    ppermute x2, waiting for transfers between devices, local(): lax.ppermute(square, 'gz', [(dev, dev ^ hop) for dev in range(4)])  270 us
    scatter-add x6, other arithmetic, product_two(): summed = summed.at[:, panel_columns[:, column_slot], :].add(product)  82.1 us
    reduce_scatter x1, waiting for transfers between devices, local(): lax.psum_scatter(3.0 * on_diagonal * square - 2.0 * applied, 'gy', scatte...  52.9 us
    dot_general x6, matrix products, product_one(): jnp.einsum('rix,iyx->riy', picked, panel_tiles[:, column_slot], preferred...  33.1 us
    psum x1, waiting for transfers between devices, broadcast(): return lax.psum(kept, axis)  27.4 us
    dot_general x6, matrix products, product_two(): jnp.einsum('rix,ixy->riy', rounded, panel_tiles[:, column_slot], preferre...  20.9 us
    unnamed x21, local copies, waits for them, and re-layouts  14.4 us
    gather x6, local copies, waits for them, and re-layouts, product_one(): picked = jnp.take(left_panel, panel_columns[:, column_slot], axis=1)  12.9 us
  transfers between devices with their start and end apart: 5, of which 4 were waited for; matrix products, arithmetic and copies ran while one was open for 4% of the time, Pallas kernels for 0%

profile of v1, /device:TPU:0, one launch (start us, length us, event | category | flops | bytes accessed | tf_op | source)
XLA Modules:
  0.0 578.1 jit_solution(13406000915250763816)
XLA Ops:
  9.2 8.0 %copy.55 = bf16[1,32,1,6,128,128]{5,4,1,3,2,0:T(8,128)(2,1)} copy(bf16[1,32,1,6,128,128]{5,4,3,2,1,0:T(8,128)(2,1)} %param.4) | data formatting | bytes 12582912 | tf_op args[0]
  18.2 8.9 %psum.18 = s32[6]{0:T(128)S(1)} all-reduce(s32[6]{0:T(128)S(1)} %fusion.44), channel_id=1, replica_groups=mesh['gx'=2,'gy'=4,'gz'=4] {'gy'}, use_global_device_ids=true, to_apply=%region_1.2 | all-reduce | flops 6 | bytes 48 | tf_op jit(solution)/shard_map/psum | solution.py:11
  29.5 27.4 %all-reduce.2.cloned.1.call-done = bf16[6,128,128]{2,0,1:T(8,128)(2,1)} async-done(((bf16[6,128,128]{2,0,1:T(8,128)(2,1)}), bf16[6,128,128]{2,0,1:T(8,128)(2,1)}) %all-reduce.2.cloned.1.call-update) | async-done | bytes 196624 | tf_op jit(solution)/shard_map/psum | solution.py:11
  73.0 6.2 %fusion.1 = f32[64,128,128]{1,2,0:T(8,128)} fusion(bf16[64,128,128]{2,1,0:T(8,128)(2,1)} %gather_fusion.4, pred[64]{0:T(512)(128)(4,1)S(1)} %get-tuple-element.24, bf16[64,6,128,128]{3,2,0,1:T(8,128)(2,1)} %bitcast.78), kind=kOutput, calls=%fused_computation.21 | convolution fusion | flops 269484032 | bytes 8388672 | tf_op jit(solution)/shard_map/rix,iyx->riy/dot_general | solution.py:31
  79.1 6.0 %fusion.3 = f32[64,128,128]{1,2,0:T(8,128)} fusion(bf16[64,128,128]{2,1,0:T(8,128)(2,1)} %gather_fusion.3, pred[64]{0:T(512)(128)(4,1)S(1)} %get-tuple-element.25, bf16[64,6,128,128]{3,2,0,1:T(8,128)(2,1)} %bitcast.79), kind=kOutput, calls=%fused_computation.23 | convolution fusion | flops 269484032 | bytes 8388672 | tf_op jit(solution)/shard_map/rix,iyx->riy/dot_general | solution.py:31
  88.8 3.6 fusion.7
  96.0 10.1 %add_add_fusion = f32[64,128,128]{1,2,0:T(8,128)} fusion(f32[64,128,128]{1,2,0:T(8,128)} %fusion.1, f32[64,128,128]{1,2,0:T(8,128)} %fusion.3, f32[64,128,128]{1,2,0:T(8,128)} %fusion.5, f32[64,128,128]{1,2,0:T(8,128)} %fusion.9, f32[64,128,128]{1,2,0:T(8,128)} %fusion.7, bf16[64,128,128]{2,1,0:T(8,128)(2,1)S(1)} %copy-done.4, ...), kind=kOutput, calls=%fused_computation.13 | convolution fusion | flops 274726912 | bytes 29360640 | tf_op jit(solution)/shard_map/rix,iyx->riy/dot_general | solution.py:31
  107.6 90.6 %collective-permute-done = f32[128,8192]{0,1:T(8,128)S(1)} collective-permute-done((f32[128,8192]{0,1:T(8,128)}, f32[128,8192]{0,1:T(8,128)S(1)}, u32[]{:S(2)}, u32[]{:S(2)}) %collective-permute-start) | collective-permute-done | bytes 4194336 | tf_op jit(solution)/shard_map/ppermute | solution.py:67
  198.2 4.7 bitcast_add_fusion
  205.2 179.7 %collective-permute-done.1 = f32[128,8192]{0,1:T(8,128)} collective-permute-done((f32[128,8192]{0,1:T(8,128)}, f32[128,8192]{0,1:T(8,128)}, u32[]{:S(2)}, u32[]{:S(2)}) %collective-permute-start.1) | collective-permute-done | bytes 4194336 | tf_op jit(solution)/shard_map/ppermute | solution.py:67
  384.9 4.0 add_convert_fusion
  389.0 5.2 fusion.24
  394.2 4.4 fusion.23
  412.5 13.7 %scatter_fusion = f32[128,64,128]{2,0,1:T(8,128)} fusion(f32[128,64,128]{2,0,1:T(8,128)} %broadcast_in_dim.30, s32[64]{0:T(128)S(1)} %get-tuple-element.7, f32[64,128,128]{2,1,0:T(8,128)} %fusion.23), kind=kCustom, calls=%fused_computation.6 | custom fusion | flops 1048576 | bytes 12583168 | tf_op jit(solution)/shard_map/scatter-add | solution.py:43
  426.2 13.6 %scatter_fusion.1 = f32[128,64,128]{2,0,1:T(8,128)} fusion(f32[128,64,128]{2,0,1:T(8,128)} %scatter_fusion, s32[64]{0:T(128)S(1)} %get-tuple-element.8, f32[64,128,128]{2,1,0:T(8,128)} %fusion.24), kind=kCustom, calls=%fused_computation.7 | custom fusion | flops 1048576 | bytes 12583168 | tf_op jit(solution)/shard_map/scatter-add | solution.py:43
  439.8 13.6 %scatter_fusion.2 = f32[128,64,128]{2,0,1:T(8,128)} fusion(f32[128,64,128]{2,0,1:T(8,128)} %scatter_fusion.1, s32[64]{0:T(128)S(1)} %get-tuple-element.9, f32[64,128,128]{2,1,0:T(8,128)} %fusion.25), kind=kCustom, calls=%fused_computation.8 | custom fusion | flops 1048576 | bytes 12583168 | tf_op jit(solution)/shard_map/scatter-add | solution.py:43
  453.4 13.6 %scatter_fusion.3 = f32[128,64,128]{2,0,1:T(8,128)} fusion(f32[128,64,128]{2,0,1:T(8,128)} %scatter_fusion.2, s32[64]{0:T(128)S(1)} %get-tuple-element.10, f32[64,128,128]{2,1,0:T(8,128)} %fusion.26), kind=kCustom, calls=%fused_computation.9 | custom fusion | flops 1048576 | bytes 12583168 | tf_op jit(solution)/shard_map/scatter-add | solution.py:43
  467.0 13.7 %scatter_fusion.4 = f32[128,64,128]{2,0,1:T(8,128)} fusion(f32[128,64,128]{2,0,1:T(8,128)} %scatter_fusion.3, s32[64]{0:T(128)S(1)} %get-tuple-element.11, f32[64,128,128]{2,1,0:T(8,128)} %fusion.27), kind=kCustom, calls=%fused_computation.10 | custom fusion | flops 1048576 | bytes 12583168 | tf_op jit(solution)/shard_map/scatter-add | solution.py:43
  480.7 13.8 %scatter_fusion.5 = f32[128,64,128]{2,0,1:T(8,128)} fusion(f32[128,64,128]{2,0,1:T(8,128)} %scatter_fusion.4, s32[64]{0:T(128)S(1)} %get-tuple-element.6, f32[64,128,128]{2,1,0:T(8,128)} %fusion.28), kind=kCustom, calls=%fused_computation.11 | custom fusion | flops 1048576 | bytes 12583168 | tf_op jit(solution)/shard_map/scatter-add | solution.py:43
  494.6 4.7 broadcast_multiply_fusion
  499.3 5.6 copy.67
  504.9 7.2 %bitcast_subtract_fusion = f32[128,8192]{0,1:T(8,128)} fusion(f32[128,64,128]{0,2,1:T(8,128)} %copy.67, f32[]{:T(128)S(6)} %mul_shard_map.3, f32[128,8192]{0,1:T(8,128)} %bitcast_add_fusion, f32[128,8192]{0,1:T(8,128)} %collective-permute-done.1), kind=kLoop, calls=%fused_computation.12 | loop fusion | flops 3145728 | bytes 16777220 | tf_op jit(solution)/shard_map/sub | solution.py:73
  512.1 5.6 copy.75
  517.8 52.9 %reduce-scatter.4.cloned.1.call-done = f32[32,8192]{1,0:T(8,128)} async-done(((f32[128,8192]{1,0:T(8,128)}), f32[32,8192]{1,0:T(8,128)}) %reduce-scatter.4.cloned.1.call-update) | async-done | bytes 1048592 | tf_op jit(solution)/shard_map/reduce_scatter | solution.py:72
  (62 shorter events, 46.1 us)
Async XLA Ops:
  7.4 49.5 %all-reduce.2.cloned.1.call-start = ((), (), s32[]{:S(2)}) async-start(), calls=%async_computation.1 | async-start | bytes 524288 | tf_op jit(solution)/shard_map/psum | solution.py:11
  9.2 63.8 %all-gather.4.cloned.1.call-start = ((), (), s32[]{:S(2)}) async-start(), calls=%async_computation.2 | async-start | bytes 18874368 | tf_op jit(solution)/shard_map/all_gather | solution.py:60
  17.3 0.7 copy-start.5
  17.3 553.4 %reduce-scatter.4.cloned.1.call-start = ((), (), s32[]{:S(2)}) async-start(), calls=%async_computation.3 | async-start | bytes 5242880 | tf_op jit(solution)/shard_map/reduce_scatter | solution.py:72
  73.0 12.2 %copy-start = (bf16[1,64,1,6,128,128]{5,4,1,3,2,0:T(8,128)(2,1)S(1)}, bf16[1,64,1,6,128,128]{5,4,1,3,2,0:T(8,128)(2,1)}, u32[]{:S(2)}) copy-start(bf16[1,64,1,6,128,128]{5,4,1,3,2,0:T(8,128)(2,1)} %all-gather.4.cloned.1.call-done) | copy-start | bytes 37748740
  79.1 6.0 %copy-start.3 = (bf16[64,128,128]{2,1,0:T(8,128)(2,1)S(1)}, bf16[64,128,128]{2,1,0:T(8,128)(2,1)}, u32[]{:S(2)}) copy-start(bf16[64,128,128]{2,1,0:T(8,128)(2,1)} %gather_fusion.2) | copy-start | bytes 6291460
  85.2 3.6 copy-start.2
  88.8 3.6 copy-start.1
  92.4 3.6 copy-start.4
  106.1 92.1 %collective-permute-start = (f32[128,8192]{0,1:T(8,128)}, f32[128,8192]{0,1:T(8,128)S(1)}, u32[]{:S(2)}, u32[]{:S(2)}) collective-permute-start(f32[128,8192]{0,1:T(8,128)} %bitcast.92), channel_id=1, source_target_pairs={{0,1},{1,0},{2,3},{3,2},{4,5},{5,4},{6,7},{7,6},{8,9},{9,8},{10,11... | collective-permute-start | bytes 12582920 | tf_op jit(solution)/shard_map/ppermute | solution.py:67
  202.9 182.1 %collective-permute-start.1 = (f32[128,8192]{0,1:T(8,128)}, f32[128,8192]{0,1:T(8,128)}, u32[]{:S(2)}, u32[]{:S(2)}) collective-permute-start(f32[128,8192]{0,1:T(8,128)} %bitcast_add_fusion), channel_id=1, source_target_pairs={{0,2},{1,3},{2,0},{3,1},{4,6},{5,7},{6,4},{7,5},{8,10},{9,11},{10,... | collective-permute-start | bytes 12582920 | tf_op jit(solution)/shard_map/ppermute | solution.py:67
  384.9 13.7 %slice-start = ((s8[12582912]{0:T(1024)(128)(4,1)}), s8[4194304]{0:T(1024)(128)(4,1)S(1)}, s32[]{:S(2)}) async-start(s8[12582912]{0:T(1024)(128)(4,1)} %bitcast.86), calls=%async_computation.4 | async-start | bytes 8388608
  384.9 13.7 %slice-start.1 = ((s8[12582912]{0:T(1024)(128)(4,1)}), s8[4194304]{0:T(1024)(128)(4,1)S(1)}, s32[]{:S(2)}) async-start(s8[12582912]{0:T(1024)(128)(4,1)} %bitcast.86), calls=%async_computation.5 | async-start | bytes 8388608
  389.0 9.7 %slice-start.2 = ((s8[12582912]{0:T(1024)(128)(4,1)}), s8[4194304]{0:T(1024)(128)(4,1)S(1)}, s32[]{:S(2)}) async-start(s8[12582912]{0:T(1024)(128)(4,1)} %bitcast.86), calls=%async_computation.6 | async-start | bytes 8388608
Sparse Core Ops, SparseCore 0:
  11.1 45.7 all-reduce.1
  517.9 52.7 reduce-scatter.3
Sparse Core Ops, SparseCore 1:
  17.4 27.3 all-gather.3
